TPU v7x, 512 devices: a whole 4x4x16 slice. The times are simulated.
512 devices in a mesh: brick: 128 (over x, z, core), chan: 4 (over y).
Axes of the slice: x: 4, y: 4, z: 16, core: 2. Of those that a mesh axis runs over, the one named last changes fastest.
Arguments:
- features: bfloat16 [512, 128, 512], P('brick', 'chan'), may hold values from -6 to 6
- fine_links: int32 [512, 26], P('brick'), may hold values from -1 to 511, as said below
- coarse_links: int32 [256, 26], P('brick'), may hold values from -1 to 255, as said below
- parents: int32 [512], P('brick'), may hold values from 0 to 2047, as said below
- down_weight: bfloat16 [8, 128, 128], P(None, None, 'chan'), may hold values from -0.1875 to 0.1875
- coarse_weight: bfloat16 [27, 128, 128], P(None, 'chan'), may hold values from -0.109375 to 0.109375
- up_weight: bfloat16 [8, 128, 128], P(None, 'chan'), may hold values from -0.5 to 0.5
- fine_weight: bfloat16 [27, 128, 128], P(None, 'chan'), may hold values from -0.109375 to 0.109375
- coarse_bias: float32 [128], P('chan'), may hold values from -3 to 3
- fine_bias: float32 [128], P('chan'), may hold values from -3 to 3
Outputs:
- refined: bfloat16 [512, 128, 512], P('brick', 'chan')
Inputs may be any that keep to these rules, and one draw needn't show every extreme that they name: `fine_links`: A fine brick's index is its owner times 4 plus its place there; the owner of fine brick b is b // 4. Among the rows of one owner's bricks, at most 1 of the entries in columns 0 to 5 name bricks of any one owner, and at most 1 of the entries in columns 6 to 25 do. `coarse_links`: A coarse brick's index is its owner times 2 plus its place there. Among the rows of one owner's coarse bricks, at most 1 of the entries in columns 0 to 5 name coarse bricks of any one owner, and at most 1 of the entries in columns 6 to 25 do. parents[b] // 8 is a coarse brick; at most 1 of one owner's fine bricks have parents on any one owner.
All inputs are finite; a program needn't handle non-finite values.
Results may differ from a plain program's by a relative error of at most 0.0059.
Values may be sent and summed in bfloat16 or wider, within the bound.
A program may use at most 64 MiB of HBM per device.

v0:
```python
import functools

import jax
import jax.numpy as jnp
import numpy as np
from jax import lax
from jax.experimental import pallas as pl
from jax.experimental.pallas import tpu as pltpu
from jax.sharding import PartitionSpec as P

EDGE = 8
NX, NZ, NC = 4, 16, 2
PEERS = NX * NZ * NC
NY = 4
HALO = 144
MESH = pl.DeviceIdType.MESH
BF16 = jnp.bfloat16
F32 = jnp.float32


def headings():
    faces = [(1, 0, 0), (-1, 0, 0), (0, 1, 0), (0, -1, 0), (0, 0, 1), (0, 0, -1)]
    steps = [(a, b, c) for a in (-1, 0, 1) for b in (-1, 0, 1) for c in (-1, 0, 1)]
    return faces + [d for d in steps if sum(map(abs, d)) >= 2]


NUMBER = {d: k for k, d in enumerate(headings())}


def inner_row(fine, cell):
    if fine:
        low = [c // 2 for c in cell]
        part = [c % 2 for c in cell]
    else:
        low = [c % 4 for c in cell]
        part = [c // 4 for c in cell]
    return low[0], (4 * part[0] + 2 * part[1] + part[2]) * 16 + low[1] * 4 + low[2]


def halo_row(d, cell):
    k = NUMBER[d]
    free = [cell[n] for n in range(3) if d[n] == 0]
    if len(free) == 2:
        return free[0] // 2, 16 * k + (free[0] % 2) * 8 + free[1]
    if len(free) == 1:
        return free[0] // 2, 96 + 2 * (k - 6) + free[0] % 2
    return 0, 96 + 2 * (k - 6)


def frame_planes(fine, j):
    return [2 * j + n for n in range(4)] if fine else [j, j + 1, j + 2, j + 4, j + 5, j + 6]


def frame_tables(fine):
    inner, outer = [], []
    for j in range(NY):
        rows_in, rows_out = [], []
        for a3 in range(3):
            for px in frame_planes(fine, j):
                for py in range(10):
                    for z in range(8):
                        at = (px, py, z + a3)
                        d = tuple(1 if v == 9 else -1 if v == 0 else 0 for v in at)
                        cell = tuple(v - 1 for v in at)
                        if d == (0, 0, 0):
                            q, r = inner_row(fine, cell)
                            rows_in.append(q * 128 + r)
                            rows_out.append(-1)
                        else:
                            q, r = halo_row(d, cell)
                            rows_in.append(-1)
                            rows_out.append(q * HALO + r)
        inner.append(rows_in)
        outer.append(rows_out)
    return np.array(inner, np.int32), np.array(outer, np.int32)


def piece_tables(fine):
    table = np.full((NY, HALO), -1, np.int32)
    for d in headings():
        edge = [0 if v == 1 else 7 for v in d]
        spans = [range(8) if v == 0 else (e,) for v, e in zip(d, edge)]
        for x in spans[0]:
            for y in spans[1]:
                for z in spans[2]:
                    cell = (x, y, z)
                    quarter, row = halo_row(d, cell)
                    q, r = inner_row(fine, cell)
                    table[quarter, row] = q * 128 + r
    return table


def unfold_table():
    rows = []
    for o in range(8):
        for u in range(16):
            x, y, z = o // 4, 2 * (u // 4) + (o // 2) % 2, 2 * (u % 4) + o % 2
            rows.append(x * 64 + y * 8 + z)
    return np.array(rows, np.int32)


def octant_table():
    rows = []
    for q in range(4):
        for u in range(16):
            rows.append((4 * (q // 2) + u // 4) * 8 + 4 * (q % 2) + u % 4)
    return np.array(rows, np.int32)


def picks(rows, width):
    return (rows[..., None] == jnp.arange(width, dtype=jnp.int32)).astype(BF16)


def place(owner):
    return owner // (NZ * NC), (owner // NC) % NZ, owner % NC


def shift_of(slot):
    j = slot // 8
    dz = jnp.where(j % 2 == 1, (j + 1) // 2, (NZ - j // 2) % NZ)
    return (slot % 8) // 2, dz, slot % 2


def dest_of(me, slot):
    x, z, c = place(me)
    dx, dz, dc = shift_of(slot)
    return ((x + dx) % NX * NZ + (z + dz) % NZ) * NC + (c + dc) % NC


def slot_from(me, owner):
    x, z, c = place(me)
    ox, oz, oc = place(owner)
    dx, dz, dc = (x - ox) % NX, (z - oz) % NZ, (c - oc) % NC
    j = jnp.where(dz == 0, 0, jnp.where(dz <= NZ // 2, 2 * dz - 1, 2 * (NZ - dz)))
    return j * 8 + dx * 2 + dc


def answer_slot(slot):
    j = slot // 8
    back = jnp.where(j == 0, 0, jnp.where(j == NZ - 1, j, jnp.where(j % 2 == 1, j + 1, j - 1)))
    return back * 8 + (NX - (slot % 8) // 2) % NX * 2 + slot % 2


AT_CHILD, AT_FF, AT_FR, AT_CF, AT_CR, AT_PAR, TABLE = 0, 128, 152, 232, 244, 284, 288

Y_FEAT, Y_DOWN, Y_BIAS, Y_UP, Y_CW, Y_FW, Y_CG, Y_CH, Y_MG, Y_FH, Y_OUT = range(11)
B_IDX, B_UP, B_CF, B_CR, B_DOWN, B_FF, B_FR = range(7)


def nt(a, b):
    return lax.dot_general(a, b, (((1,), (1,)), ((), ())), preferred_element_type=F32)


def nn(a, b):
    return jnp.dot(a, b, preferred_element_type=F32)


def kernel(
    table, feat, idx_send, down_w, up_w, coarse_w, fine_w, bias, unfold, octant,
    coarse_pick, fine_pick, coarse_inner, coarse_outer, fine_inner, fine_outer,
    out,
    idx_recv, idx_smem, feats, down_all, bias_all, up_all, coarse_w_all, fine_w_all,
    own, child, up_send, up_recv, coarse_all, faces, rims, cf_send, cr_send, cf_recv, cr_recv,
    coarse_halo, frame, columns, octants, down_send, down_recv, merged_all, ff_send, fr_send,
    ff_recv, fr_recv, fine_halo, rim_rows, out_send, out_recv,
    y_ss, y_rs, b_ss, b_rs, local_sem,
):
    me, y = lax.axis_index("brick"), lax.axis_index("chan")

    barrier = pltpu.get_barrier_semaphore()

    def greet(s, carry):
        pl.semaphore_signal(barrier, inc=1, device_id={"brick": dest_of(me, s)}, device_id_type=MESH)
        return carry

    lax.fori_loop(1, PEERS, greet, 0)
    for k in range(1, NY):
        pl.semaphore_signal(barrier, inc=1, device_id={"chan": (y + k) % NY}, device_id_type=MESH)
    pl.semaphore_wait(barrier, PEERS - 1 + NY - 1)

    def y_copies(phase, src, dst):
        return [
            pltpu.make_async_remote_copy(
                src_ref=src((y + k) % NY), dst_ref=dst, send_sem=y_ss.at[phase, k - 1],
                recv_sem=y_rs.at[phase, k - 1], device_id={"chan": (y + k) % NY}, device_id_type=MESH,
            )
            for k in range(1, NY)
        ]

    def y_start(copies):
        for c in copies:
            c.start()

    def y_arrived(copies):
        for c in copies:
            c.wait_recv()

    def b_copy(phase, src, dst, s):
        return pltpu.make_async_remote_copy(
            src_ref=src.at[s], dst_ref=dst.at[s], send_sem=b_ss.at[phase], recv_sem=b_rs.at[phase],
            device_id={"brick": dest_of(me, s)}, device_id_type=MESH,
        )

    def b_all(phase, src, dst):
        return pltpu.make_async_remote_copy(
            src_ref=src.at[pl.ds(1, PEERS - 1)], dst_ref=dst.at[pl.ds(1, PEERS - 1)],
            send_sem=b_ss.at[phase], recv_sem=b_rs.at[phase],
            device_id={"brick": dest_of(me, 1)}, device_id_type=MESH,
        )

    def b_start(*exchanges):
        def send(t, carry):
            for phase, src, dst in exchanges:
                b_copy(phase, src, dst, PEERS - 1 - t).start()
            return carry

        lax.fori_loop(0, PEERS - 1, send, 0)

    def mine(ref):
        return ref.at[y]

    feat_copies = y_copies(Y_FEAT, lambda p: feat.at[:, :, pl.ds(pl.multiple_of(p * 128, 128), 128)],
                           feats.at[:, pl.ds(pl.multiple_of(y * 32, 32), 32), :])
    y_start(feat_copies)
    down_copies = y_copies(Y_DOWN, lambda p: down_w, mine(down_all))
    y_start(down_copies)
    b_start((B_IDX, idx_send, idx_recv))
    later = []
    for phase, src, dst in ((Y_BIAS, bias, bias_all), (Y_CW, coarse_w, coarse_w_all),
                            (Y_UP, up_w, up_all), (Y_FW, fine_w, fine_w_all)):
        copies = y_copies(phase, lambda p, src=src: src, mine(dst))
        y_start(copies)
        later.append(copies)
    feats[:, pl.ds(pl.multiple_of(y * 32, 32), 32), :] = (
        feat[:, :, pl.ds(pl.multiple_of(y * 128, 128), 128)])
    down_all[y] = down_w[...]
    bias_all[y] = bias[...]
    coarse_w_all[y] = coarse_w[...]
    up_all[y] = up_w[...]
    fine_w_all[y] = fine_w[...]
    idx_recv[0] = idx_send[0]

    y_arrived(feat_copies)
    y_arrived(down_copies)
    for b in range(4):
        own[b] = nt(unfold[...], feats[b]).astype(BF16)
    total = jnp.zeros((64, 128), F32)
    for o in range(8):
        rows = jnp.concatenate([own[b, 16 * o:16 * o + 16, :] for b in range(4)], axis=0)
        weight = jnp.concatenate([down_all[i, o] for i in range(NY)], axis=0)
        total = total + nn(rows, weight)
    child[...] = total.astype(BF16).reshape(4, 16, 128)

    def give_child(t, carry):
        s = PEERS - 1 - t
        up_send[s] = child[table[AT_CHILD + s]]
        return carry

    lax.fori_loop(0, PEERS, give_child, 0, unroll=4)
    b_start((B_UP, up_send, up_recv))
    up_recv[0] = up_send[0]

    zero = jnp.zeros((16, 128), BF16)
    for ref in (cf_recv, ff_recv):
        ref[PEERS] = zero
    for ref in (cr_recv, fr_recv):
        ref[PEERS] = jnp.zeros((2, 128), BF16)
    rim_rows[...] = jnp.zeros(rim_rows.shape, F32)

    idx_all = b_all(B_IDX, idx_send, idx_recv)
    idx_all.wait_recv()
    to_smem = pltpu.make_async_copy(idx_recv, idx_smem, local_sem)
    to_smem.start()
    to_smem.wait()

    up_done = b_all(B_UP, up_send, up_recv)
    up_done.wait_recv()
    row = lax.broadcasted_iota(jnp.int32, (256, 128), 0)
    lane = lax.broadcasted_iota(jnp.int32, (256, 128), 1)
    same = row % 16 == lane % 16
    wide = lax.broadcasted_iota(jnp.int32, (1, 128), 1) // 16

    def add_children(g, acc):
        codes = jnp.zeros((1, 128), jnp.int32)
        for i in range(8):
            codes = jnp.where(wide == i, idx_smem[8 * g + i, 0, 4], codes)
        hot = jnp.where(same & (row // 16 == codes), 1.0, 0.0).astype(BF16)
        return acc + nn(hot, up_recv[pl.ds(8 * g, 8)].reshape(128, 128))

    summed = lax.fori_loop(0, PEERS // 8, add_children, jnp.zeros((256, 128), F32))
    coarse_all[y] = summed.astype(BF16).reshape(2, 128, 128)
    gather = y_copies(Y_CG, lambda p: mine(coarse_all), mine(coarse_all))
    y_start(gather)
    y_arrived(gather)

    def halo(bricks, whole, pick, f_field, at_f, at_r, f_phase, r_phase, y_phase,
             f_send, r_send, f_recv, r_recv, halo_all, inner, outer, rows):
        for b in range(bricks):
            source = jnp.concatenate([whole[i, b] for i in range(NY)], axis=0)
            found = nn(pick[...], source)
            faces[pl.ds(6 * b, 6)] = found[:96].astype(BF16).reshape(6, 16, 128)
            for r in range(20):
                rims[20 * b + r] = found[96 + 2 * r:98 + 2 * r].astype(BF16)

        def answer(t, carry):
            s = PEERS - 1 - t
            asker = answer_slot(s)
            f_send[s] = faces[idx_smem[asker, 0, f_field]]
            r_send[s] = rims[idx_smem[asker, 0, f_field + 1]]
            return carry

        lax.fori_loop(0, PEERS, answer, 0, unroll=4)
        b_start((f_phase, f_send, f_recv), (r_phase, r_send, r_recv))
        f_recv[0] = f_send[0]
        r_recv[0] = r_send[0]
        for b in range(bricks):
            source = jnp.concatenate([whole[i, b] for i in range(NY)], axis=0)
            frame[b, 0:rows, :] = nn(inner[...], source)
        waits = [b_all(f_phase, f_send, f_recv), b_all(r_phase, r_send, r_recv)]
        for w in waits:
            w.wait_recv()
        for b in range(bricks):
            for k in range(6):
                halo_all[y, b, 16 * k:16 * k + 16, :] = f_recv[table[at_f + 6 * b + k]]
            for r in range(20):
                rim_rows[b, 2 * r:2 * r + 2, :] = r_recv[table[at_r + 20 * b + r]].astype(F32)
            halo_all[y, b, 96:144, :] = rim_rows[b].astype(BF16)
        around = y_copies(y_phase, lambda p: mine(halo_all), mine(halo_all))
        y_start(around)
        y_arrived(around)
        for b in range(bricks):
            source = jnp.concatenate([halo_all[i, b] for i in range(NY)], axis=0)
            frame[b, 0:rows, :] = frame[b, 0:rows, :] + nn(outer[...], source)
        return waits, around

    def conv(bricks, planes, starts, weights, bias_row):
        for tap in range(27):
            a, a2, a3 = tap // 9, (tap // 3) % 3, tap % 3
            for b in range(bricks):
                for n, start in enumerate(starts):
                    at = ((a3 * planes + start + a) * 10 + a2) * 8
                    columns[(2 * b + n) * 64:(2 * b + n + 1) * 64, tap * 128:tap * 128 + 128] = (
                        frame[b, at:at + 64, :].astype(BF16))
        weight = jnp.concatenate([weights[i] for i in range(NY)], axis=0)
        whole = nt(columns[0:bricks * 128, :], weight)
        shift = bias_all[0] + bias_all[1] + bias_all[2] + bias_all[3]
        return jnp.maximum(whole + shift[bias_row:bias_row + 1, :], 0.0)

    coarse_waits, coarse_around = halo(
        2, coarse_all, coarse_pick, 2, AT_CF, AT_CR, B_CF, B_CR, Y_CH,
        cf_send, cr_send, cf_recv, cr_recv, coarse_halo, coarse_inner, coarse_outer, 1440)
    for copies in later:
        y_arrived(copies)
    coarse_out = conv(2, 6, (0, 3), coarse_w_all, 0).astype(BF16)
    for p in range(2):
        for n in range(2):
            at = (2 * p + n) * 64
            octants[pl.ds(8 * p + 4 * n, 4)] = (
                nn(octant[...], coarse_out[at:at + 64]).astype(BF16).reshape(4, 16, 128))

    def give_octant(t, carry):
        s = PEERS - 1 - t
        down_send[s] = octants[jnp.maximum(idx_smem[answer_slot(s), 0, 4], 0)]
        return carry

    lax.fori_loop(0, PEERS, give_octant, 0, unroll=4)
    b_start((B_DOWN, down_send, down_recv))
    down_recv[0] = down_send[0]
    down_done = b_all(B_DOWN, down_send, down_recv)
    down_done.wait_recv()
    coarse_rows = jnp.concatenate([down_recv[table[AT_PAR + b]] for b in range(4)], axis=0)
    for o in range(8):
        weight = jnp.concatenate([up_all[i, o] for i in range(NY)], axis=0)
        lifted = nt(coarse_rows, weight)
        for b in range(4):
            merged_all[y, b, 16 * o:16 * o + 16, :] = (
                own[b, 16 * o:16 * o + 16, :].astype(F32) + lifted[16 * b:16 * b + 16]).astype(BF16)
    merge = y_copies(Y_MG, lambda p: mine(merged_all), mine(merged_all))
    y_start(merge)
    y_arrived(merge)

    fine_waits, fine_around = halo(
        4, merged_all, fine_pick, 0, AT_FF, AT_FR, B_FF, B_FR, Y_FH,
        ff_send, fr_send, ff_recv, fr_recv, fine_halo, fine_inner, fine_outer, 960)
    refined = conv(4, 4, (0, 1), fine_w_all, 1)
    for b in range(4):
        out_send[b] = refined[128 * b:128 * b + 128].T.astype(BF16)
    back = y_copies(Y_OUT, lambda p: out_send.at[:, pl.ds(pl.multiple_of(p * 32, 32), 32), :],
                    mine(out_recv))
    y_start(back)
    out_recv[y] = out_send[:, pl.ds(pl.multiple_of(y * 32, 32), 32), :]
    y_arrived(back)
    for i in range(NY):
        out[:, :, 128 * i:128 * i + 128] = out_recv[i]

    for w in [idx_all, up_done, down_done] + coarse_waits + fine_waits:
        w.wait_send()
    for copies in [feat_copies, down_copies, gather, coarse_around, merge, fine_around, back] + later:
        for c in copies:
            c.wait_send()


def requests(links, per_owner, dest):
    listed = links.reshape(1, -1)
    number = jnp.arange(links.shape[1], dtype=jnp.int32)[None, :]
    wanted = (links % per_owner * links.shape[1] + number).reshape(1, -1)
    hit = (listed >= 0) & (listed // per_owner == dest[:, None])
    return jnp.sum(jnp.where(hit, wanted, 0), axis=1)


def per_device(features, fine_links, coarse_links, parents, down_weight, coarse_weight, up_weight,
               fine_weight, coarse_bias, fine_bias):
    me, y = lax.axis_index("brick"), lax.axis_index("chan")
    dest = dest_of(me, jnp.arange(PEERS, dtype=jnp.int32))
    home = parents // 16
    there = home[None, :] == dest[:, None]
    code = jnp.sum(jnp.where(there, parents[None, :] % 16 + 1, 0), axis=1) - 1
    child = jnp.sum(jnp.where(there, jnp.arange(4, dtype=jnp.int32)[None, :], 0), axis=1)
    ask = jnp.stack([
        requests(fine_links[:, :6], 4, dest), requests(fine_links[:, 6:], 4, dest),
        requests(coarse_links[:, :6], 2, dest), requests(coarse_links[:, 6:], 2, dest), code], axis=1)
    idx_send = jnp.pad(ask, ((0, 0), (0, 123)))[:, None, :]

    def found(links, per_owner):
        flat = links.reshape(-1)
        return jnp.where(flat >= 0, slot_from(me, flat // per_owner), PEERS)

    table = jnp.concatenate([
        child, found(fine_links[:, :6], 4), found(fine_links[:, 6:], 4),
        found(coarse_links[:, :6], 2), found(coarse_links[:, 6:], 2), slot_from(me, home)])
    ci, co = frame_tables(False)
    fi, fo = frame_tables(True)
    mine = lambda t: lax.dynamic_index_in_dim(jnp.asarray(t), y, 0, keepdims=False)
    bias = jnp.stack([coarse_bias, fine_bias])
    bias = lax.dynamic_update_slice(jnp.zeros((8, 128), F32), bias, (0, y * 32))
    args = (
        table, features, idx_send,
        jnp.transpose(down_weight, (0, 2, 1)), up_weight,
        jnp.transpose(coarse_weight, (1, 0, 2)).reshape(32, 27 * 128),
        jnp.transpose(fine_weight, (1, 0, 2)).reshape(32, 27 * 128), bias,
        picks(jnp.asarray(unfold_table()), 128), picks(jnp.asarray(octant_table()), 64),
        picks(mine(piece_tables(False)), 512), picks(mine(piece_tables(True)), 512),
        picks(mine(ci), 512), picks(mine(co), 4 * HALO), picks(mine(fi), 512), picks(mine(fo), 4 * HALO),
    )
    v = pltpu.VMEM
    scratch = dict(
        idx_recv=v((128, 1, 128), jnp.int32), idx_smem=pltpu.SMEM((128, 1, 128), jnp.int32),
        feats=v((4, 128, 128), BF16), down_all=v((4, 8, 32, 128), BF16), bias_all=v((4, 8, 128), F32),
        up_all=v((4, 8, 32, 128), BF16), coarse_w_all=v((4, 32, 3456), BF16),
        fine_w_all=v((4, 32, 3456), BF16), own=v((4, 128, 128), BF16), child=v((4, 16, 128), BF16),
        up_send=v((128, 16, 128), BF16), up_recv=v((128, 16, 128), BF16),
        coarse_all=v((4, 2, 128, 128), BF16), faces=v((24, 16, 128), BF16), rims=v((80, 2, 128), BF16),
        cf_send=v((128, 16, 128), BF16), cr_send=v((128, 2, 128), BF16),
        cf_recv=v((129, 16, 128), BF16), cr_recv=v((129, 2, 128), BF16),
        coarse_halo=v((4, 2, HALO, 128), BF16), frame=v((4, 1440, 128), F32),
        columns=v((512, 3456), BF16), octants=v((16, 16, 128), BF16),
        down_send=v((128, 16, 128), BF16), down_recv=v((128, 16, 128), BF16),
        merged_all=v((4, 4, 128, 128), BF16),
        ff_send=v((128, 16, 128), BF16), fr_send=v((128, 2, 128), BF16),
        ff_recv=v((129, 16, 128), BF16), fr_recv=v((129, 2, 128), BF16),
        fine_halo=v((4, 4, HALO, 128), BF16), rim_rows=v((4, 48, 128), F32),
        out_send=v((4, 128, 128), BF16), out_recv=v((4, 4, 32, 128), BF16),
        y_ss=pltpu.SemaphoreType.DMA((11, 3)), y_rs=pltpu.SemaphoreType.DMA((11, 3)),
        b_ss=pltpu.SemaphoreType.DMA((7,)), b_rs=pltpu.SemaphoreType.DMA((7,)),
        local_sem=pltpu.SemaphoreType.DMA,
    )
    return pl.pallas_call(
        kernel,
        out_shape=jax.ShapeDtypeStruct((4, 32, 512), BF16),
        in_specs=[pl.BlockSpec(memory_space=pltpu.SMEM)] + [pl.BlockSpec(memory_space=v)] * 15,
        out_specs=pl.BlockSpec(memory_space=v),
        scratch_shapes=list(scratch.values()),
        compiler_params=pltpu.CompilerParams(collective_id=0, has_side_effects=True),
    )(*args)


def solution(mesh):
    in_specs = (
        P("brick", "chan", None), P("brick", None), P("brick", None), P("brick"),
        P(None, None, "chan"), P(None, "chan", None), P(None, "chan", None), P(None, "chan", None),
        P("chan"), P("chan"),
    )
    return jax.shard_map(
        per_device, mesh=mesh, in_specs=in_specs, out_specs=P("brick", "chan", None), check_vma=False
    )
```

profile of v0, /device:TPU:1, one launch (start us, length us, event | category | flops | bytes accessed | tf_op | source)
XLA Modules:
  0.0 217.6 jit_solution(17227545358966428952)
XLA Ops:
  0.0 0.0 copy-start
  0.0 0.7 pad_maximum_fusion
  0.8 0.7 fusion.28
  1.4 0.1 fusion.9
  1.5 0.7 constant_dynamic-slice_fusion
  2.3 0.7 fusion.17
  3.0 0.1 broadcast_in_dim.146
  3.0 0.1 reshape.466
  3.2 0.1 select_reduce_fusion.3
  3.3 0.8 fusion.19
  4.0 0.1 broadcast_in_dim.149
  4.1 0.1 reshape.467
  4.2 0.1 select_reduce_fusion.1
  4.3 0.3 dynamic_update_slice.3.bias
  4.7 0.0 copy-start.1
  4.7 0.7 fusion.12
  5.4 0.1 broadcast_in_dim.140
  5.5 0.1 reshape.464
  5.6 0.1 select_reduce_fusion.2
  5.7 0.8 fusion.15
  6.4 0.1 broadcast_in_dim.143
  6.5 0.1 reshape.465
  6.7 0.1 select_reduce_fusion
  6.8 0.7 concatenate.3.table
  7.5 0.7 constant_dynamic-slice_fusion.2
  8.2 0.8 dynamic-slice_reduce_fusion
  9.0 1.3 fusion.7.octant
  10.4 1.3 fusion.6.unfold
  11.7 0.1 copy.36
  11.8 0.6 pad.4
  12.4 0.8 fusion.4.coarse_pick
  13.2 0.8 fusion.5.fine_pick
  14.0 0.0 copy-done
  14.0 1.8 copy_bitcast_fusion
  15.8 1.2 fusion.3.fine_inner
  16.9 1.3 fusion.2.fine_outer
  18.3 0.0 copy-done.1
  18.3 1.4 fusion.1.coarse_inner
  19.7 1.6 fusion.coarse_outer
  21.3 194.7 %shard_map.172 = bf16[4,32,512]{2,1,0:T(8,128)(2,1)} custom-call(s32[288]{0:T(512)} %concatenate.3.table, bf16[4,32,512]{2,1,0:T(8,128)(2,1)} %feat.1, s32[128,1,128]{2,1,0:T(1,128)} %bitcast.26, bf16[8,32,128]{2,1,0:T(8,128)(2,1)} %bitcast.27, bf16[8,32,128]{2,1,0:T(8,128)(2,1)} %up_w.1, bf16[32,3456]{1,0:T(8,128)(2,1)} %get-tuple-element.33.coarse_w, ...), custom_call_target="tpu_custom_call" | custom-call | tf_op jit(solution)/shard_map/pallas_call | solution.py:467
  216.0 1.6 copy.45
  (12 shorter events, 0.2 us)
Async XLA Ops:
  0.0 14.0 %copy-start = (bf16[27,32,128]{2,1,0:T(8,128)(2,1)S(1)}, bf16[27,32,128]{2,1,0:T(8,128)(2,1)}, u32[]{:S(2)}) copy-start(bf16[27,32,128]{2,1,0:T(8,128)(2,1)} %param.23) | copy-start | bytes 663556
  4.7 13.6 %copy-start.1 = (f32[8,128]{1,0:T(8,128)}, f32[8,128]{1,0:T(8,128)S(1)}, u32[]{:S(2)}) copy-start(f32[8,128]{1,0:T(8,128)S(1)} %dynamic_update_slice.3.bias) | copy-start | bytes 12292
where the time goes:
time: 218 us
  Pallas kernels  195 us (89%)
  other arithmetic  14.8 us (7%)
  local copies, waits for them, and re-layouts  8.04 us (4%)
    pallas_call x1, Pallas kernels, per_device(): pl.pallas_call(kernel, out_shape=jax.ShapeDtypeStruct((4, 32, 512), BF16)...  195 us
    convert_element_type x8, other arithmetic, picks(): return (rows[..., None] == jnp.arange(width, dtype=jnp.int32)).astype(BF16)  9.78 us

commit v1 on v0

v1 whole, which is shorter than its diff:
```python
import functools

import jax
import jax.numpy as jnp
import numpy as np
from jax import lax
from jax.experimental import pallas as pl
from jax.experimental.pallas import tpu as pltpu
from jax.sharding import PartitionSpec as P

EDGE = 8
NX, NZ, NC = 4, 16, 2
PEERS = NX * NZ * NC
NY = 4
HALO = 144
MESH = pl.DeviceIdType.MESH
BF16 = jnp.bfloat16
F32 = jnp.float32


def headings():
    faces = [(1, 0, 0), (-1, 0, 0), (0, 1, 0), (0, -1, 0), (0, 0, 1), (0, 0, -1)]
    steps = [(a, b, c) for a in (-1, 0, 1) for b in (-1, 0, 1) for c in (-1, 0, 1)]
    return faces + [d for d in steps if sum(map(abs, d)) >= 2]


NUMBER = {d: k for k, d in enumerate(headings())}


def inner_row(fine, cell):
    if fine:
        low = [c // 2 for c in cell]
        part = [c % 2 for c in cell]
    else:
        low = [c % 4 for c in cell]
        part = [c // 4 for c in cell]
    return low[0], (4 * part[0] + 2 * part[1] + part[2]) * 16 + low[1] * 4 + low[2]


def halo_row(fine, d, cell):
    k = NUMBER[d]
    free = [cell[n] for n in range(3) if d[n] == 0]
    if not free:
        return 0, 96 + 2 * (k - 6)
    if d[0] == 0 and not fine:
        quarter, half = free[0] % 4, free[0] // 4
    else:
        quarter, half = free[0] // 2, free[0] % 2
    if len(free) == 2:
        return quarter, 16 * k + half * 8 + free[1]
    return quarter, 96 + 2 * (k - 6) + half


def frame_planes(fine, j):
    return [2 * j + n for n in range(4)] if fine else [j, j + 1, j + 2, j + 4, j + 5, j + 6]


def frame_tables(fine):
    inner, outer = [], []
    for j in range(NY):
        rows_in, rows_out = [], []
        for a3 in range(3):
            for px in frame_planes(fine, j):
                for py in range(10):
                    for z in range(8):
                        at = (px, py, z + a3)
                        d = tuple(1 if v == 9 else -1 if v == 0 else 0 for v in at)
                        cell = tuple(v - 1 for v in at)
                        if d == (0, 0, 0):
                            q, r = inner_row(fine, cell)
                            rows_in.append(q * 128 + r)
                            rows_out.append(-1)
                        else:
                            q, r = halo_row(fine, d, cell)
                            rows_in.append(-1)
                            rows_out.append(q * HALO + r)
        inner.append(rows_in)
        outer.append(rows_out)
    return np.array(inner, np.int32), np.array(outer, np.int32)


def piece_tables(fine):
    table = np.full((NY, HALO), -1, np.int32)
    for d in headings():
        edge = [0 if v == 1 else 7 for v in d]
        spans = [range(8) if v == 0 else (e,) for v, e in zip(d, edge)]
        for x in spans[0]:
            for y in spans[1]:
                for z in spans[2]:
                    cell = (x, y, z)
                    quarter, row = halo_row(fine, d, cell)
                    q, r = inner_row(fine, cell)
                    if x == 0:
                        table[quarter, row] = r
                    elif x == 7:
                        table[quarter, row] = r
                    else:
                        assert q == quarter
                        table[quarter, row] = 128 + r
    return table


def unfold_table():
    rows = []
    for o in range(8):
        for u in range(16):
            x, y, z = o // 4, 2 * (u // 4) + (o // 2) % 2, 2 * (u % 4) + o % 2
            rows.append(x * 64 + y * 8 + z)
    return np.array(rows, np.int32)


def octant_table():
    rows = []
    for q in range(4):
        for u in range(16):
            rows.append((4 * (q // 2) + u // 4) * 8 + 4 * (q % 2) + u % 4)
    return np.array(rows, np.int32)


def row_tables():
    unfold = np.broadcast_to(unfold_table(), (NY, 128))
    octant = np.broadcast_to(octant_table(), (NY, 64))
    frames = []
    for fine in (False, True):
        inner, outer = frame_tables(fine)
        frames.append(np.where(inner >= 0, inner, 512 + outer))
    return np.concatenate(
        [unfold, octant, piece_tables(False), piece_tables(True), frames[0], frames[1]], axis=1)


ROW_UNFOLD, ROW_OCTANT, ROW_CP, ROW_FP, ROW_CF, ROW_FF, ROWS = 0, 128, 192, 336, 480, 1920, 2880


AT_PAR = 52

Y_FEAT, Y_DOWN, Y_BIAS, Y_UP, Y_CW, Y_FW, Y_CG, Y_CG2, Y_CH, Y_MG, Y_MG2, Y_FH, Y_OUT = range(13)
B_IDX, B_IDR, B_UP, B_CF, B_CR, B_DOWN, B_FF, B_FR = range(8)


def nt(a, b):
    return lax.dot_general(a, b, (((1,), (1,)), ((), ())), preferred_element_type=F32)


def nn(a, b):
    return jnp.dot(a, b, preferred_element_type=F32)


def within(index, count):
    return jnp.minimum(jnp.maximum(index, 0), count - 1)


def choose(values, index):
    picked = values[0]
    for n in range(1, len(values)):
        picked = jnp.where(index == n, values[n], picked)
    return picked


def kernel(
    links, feat, link_rows, down_w, up_w, coarse_w, fine_w, bias, row_of,
    out,
    notes, table, asks, idx_smem, unfold, octant, coarse_pick, fine_pick, coarse_inner, coarse_outer,
    fine_inner, fine_outer, coarse_w_flat, fine_w_flat,
    il_recv, ir_recv, feats, down_all, bias_all, up_all, coarse_w_all, fine_w_all,
    own, child, column, relay_send, up_recv, coarse_all, faces, rims, cf_send, cr_send, cf_recv, cr_recv,
    coarse_halo, frame, columns, octants, down_send, down_mid, down_out, down_recv, merged_all, ff_send, fr_send,
    ff_recv, fr_recv, fine_halo, rim_rows, out_send, out_recv,
    y_ss, y_rs, b_ss, b_rs, a_ss, a_rs, d_ss, d_rs, local_sem,
):
    me, y = lax.axis_index("brick"), lax.axis_index("chan")
    x, z, core = me // (NZ * NC), me // NC % NZ, me % NC

    near = [(x + n // 2) % NX * (NZ * NC) + (core + n % 2) % NC for n in range(8)]

    def z_base(j):
        step = (j + 1) // 2
        ahead = z + step
        back = z + NZ - j // 2
        at = (j % 2) * ahead + (1 - j % 2) * back
        return at % NZ * NC

    def pick(dst, first, base, width):
        for at in range(0, width, 128):
            w = min(128, width - at)
            lanes = lax.broadcasted_iota(jnp.int32, (dst.shape[0], w), 1) + (base + at)
            hit = row_of[first:first + dst.shape[0], 0:w] == lanes
            dst[:, at:at + w] = jnp.where(hit, 1.0, 0.0).astype(BF16)

    barrier = pltpu.get_barrier_semaphore()

    def greet(j, base, first):
        for n in range(first, 8):
            pl.semaphore_signal(barrier, inc=1, device_id={"brick": near[n] + base}, device_id_type=MESH)

    def greet_far(t, carry):
        greet(15 - t, z_base(15 - t), 0)
        return carry

    lax.fori_loop(0, 15, greet_far, 0)
    greet(0, z * NC, 1)
    for k in range(1, NY):
        pl.semaphore_signal(barrier, inc=1, device_id={"chan": (y + k) % NY}, device_id_type=MESH)

    def slots(l, owner):
        dx, dz, dc = (x - (owner >> 5)) & 3, (z - (owner >> 1)) & 15, (core - owner) & 1
        j = jnp.where(dz == 0, 0, jnp.where(dz <= 8, 2 * dz - 1, 32 - 2 * dz))
        return j, jnp.where(l >= 0, j * 8 + dx * 2 + dc, PEERS)

    lane = lax.broadcasted_iota(jnp.int32, (1, 128), 1)
    fine_row, coarse_row = link_rows[0], link_rows[1]
    _, notes[0] = slots(fine_row, fine_row >> 2)
    j, slot = slots(coarse_row, jnp.where(lane < AT_PAR, coarse_row >> 1, coarse_row >> 4))
    notes[1] = jnp.where(lane < AT_PAR, slot, j)
    to_table = pltpu.make_async_copy(notes, table, local_sem)
    to_table.start()
    to_table.wait()
    pick(unfold, ROW_UNFOLD, 0, 128)
    pl.semaphore_wait(barrier, PEERS - 1 + NY - 1)

    def y_copies(phase, src, dst):
        return [
            pltpu.make_async_remote_copy(
                src_ref=src((y + k) % NY), dst_ref=dst, send_sem=y_ss.at[phase, k - 1],
                recv_sem=y_rs.at[phase, k - 1], device_id={"chan": (y + k) % NY}, device_id_type=MESH,
            )
            for k in range(1, NY)
        ]

    def y_start(copies):
        for c in copies:
            c.start()

    def y_arrived(copies):
        for c in copies:
            c.wait_recv()

    def b_all(phase, src, dst):
        return pltpu.make_async_remote_copy(
            src_ref=src.at[pl.ds(1, PEERS - 1)], dst_ref=dst.at[pl.ds(1, PEERS - 1)],
            send_sem=b_ss.at[phase], recv_sem=b_rs.at[phase],
            device_id={"brick": near[1] + z * NC}, device_id_type=MESH,
        )

    def send_group(exchanges, j, base, first):
        for n in range(first, 8):
            for phase, src, dst in exchanges:
                pltpu.make_async_remote_copy(
                    src_ref=src(8 * j + n), dst_ref=dst.at[8 * j + n], send_sem=b_ss.at[phase],
                    recv_sem=b_rs.at[phase], device_id={"brick": near[n] + base}, device_id_type=MESH,
                ).start()

    def exchange(exchanges, fill=None):
        def group(t, carry):
            if fill is not None:
                fill(14 - t, 14 - t + (t % 2) * 2 - 1 + jnp.where(t == 14, 1, 0))
            send_group(exchanges, 15 - t, z_base(15 - t), 0)
            return carry

        if fill is not None:
            fill(15, 15)
        lax.fori_loop(0, 15, group, 0)
        send_group(exchanges, 0, z * NC, 1)

    def mine(ref):
        return ref.at[y]

    feat_copies = y_copies(Y_FEAT, lambda p: feat.at[:, :, pl.ds(pl.multiple_of(p * 128, 128), 128)],
                           feats.at[:, pl.ds(pl.multiple_of(y * 32, 32), 32), :])
    y_start(feat_copies)
    down_copies = y_copies(Y_DOWN, lambda p: down_w, mine(down_all))
    y_start(down_copies)
    exchange(((B_IDX, lambda s: link_rows.at[0], il_recv), (B_IDR, lambda s: link_rows.at[1], ir_recv)))
    later = []

    def gather_weights(*weights):
        for phase, src, dst in weights:
            copies = y_copies(phase, lambda p, src=src: src, mine(dst))
            y_start(copies)
            later.append(copies)

    gather_weights((Y_BIAS, bias, bias_all), (Y_CW, coarse_w, coarse_w_all))
    feats[:, pl.ds(pl.multiple_of(y * 32, 32), 32), :] = (
        feat[:, :, pl.ds(pl.multiple_of(y * 128, 128), 128)])
    down_all[y] = down_w[...]
    bias_all[y] = bias[...]
    coarse_w_all[y] = coarse_w[...]
    up_all[y] = up_w[...]
    fine_w_all[y] = fine_w[...]
    il_recv[0] = link_rows[0]
    ir_recv[0] = link_rows[1]

    y_arrived(feat_copies)
    y_arrived(down_copies)
    for b in range(4):
        own[b] = nt(unfold[...], feats[b]).astype(BF16)
    total = jnp.zeros((64, 128), F32)
    for o in range(8):
        rows = jnp.concatenate([own[b, 16 * o:16 * o + 16, :] for b in range(4)], axis=0)
        weight = jnp.concatenate([down_all[i, o] for i in range(NY)], axis=0)
        total = total + nn(rows, weight)
    child[...] = total.astype(BF16).reshape(4, 16, 128)

    def column_copy(j):
        return pltpu.make_async_remote_copy(
            src_ref=child, dst_ref=column.at[j], send_sem=a_ss.at[j], recv_sem=a_rs.at[j],
            device_id={"brick": near[0] + z_base(j)}, device_id_type=MESH,
        )

    for j in range(1, NZ):
        column_copy(j).start()
    column[0] = child[...]

    zero = jnp.zeros((16, 128), BF16)
    for ref in (cf_recv, ff_recv):
        ref[PEERS] = zero
    for ref in (cr_recv, fr_recv):
        ref[PEERS] = jnp.zeros((2, 128), BF16)
    rim_rows[...] = jnp.zeros(rim_rows.shape, F32)

    pick(octant, ROW_OCTANT, 0, 64)
    pick(coarse_pick, ROW_CP, 0, 256)
    pick(coarse_inner, ROW_CF, 0, 512)
    pick(coarse_outer, ROW_CF, 512, 4 * HALO)

    idx_waits = [b_all(B_IDX, il_recv, il_recv), b_all(B_IDR, ir_recv, ir_recv)]
    for w in idx_waits:
        w.wait_recv()

    at = lax.broadcasted_iota(jnp.int32, (1, 1, 128), 2)

    k = at
    for n in (104, 78, 52, 26):
        k = jnp.where(at >= n, jnp.minimum(k, at - n), k)
    face, coarse, parent = k < 6, at < AT_PAR, (at >= AT_PAR) & (at < AT_PAR + 4)
    seen = il_recv[...]
    place_in = jnp.where(face, (seen & 3) * 6 + k, (seen & 3) * 20 + (k - 6))
    fine_ask = jnp.where((seen >> 2 == me) & (at < 104), place_in, 0)
    seen = ir_recv[...]
    place_in = jnp.where(face, (seen & 1) * 6 + k, (seen & 1) * 20 + (k - 6))
    coarse_ask = jnp.where((seen >> 1 == me) & coarse, place_in, 0)
    code_ask = jnp.where((seen >> 4 == me) & parent, (seen & 15) + 1, 0)
    total_asks = jnp.zeros((PEERS, 1, 128), jnp.int32)
    for field, v in enumerate((
            jnp.where(face, fine_ask, 0), jnp.where(face, 0, fine_ask),
            jnp.where(face, coarse_ask, 0), jnp.where(face, 0, coarse_ask), code_ask)):
        got = jnp.max(v, axis=2, keepdims=True)
        total_asks = jnp.where(at == field, got - (1 if field == 4 else 0), total_asks)
    asks[0:PEERS] = total_asks
    seen = jnp.concatenate([ir_recv[8 * j:8 * j + 1] for j in range(NZ)], axis=0)
    sent = jnp.zeros((NZ, 1, 128), jnp.int32)
    for n in range(8):
        v = jnp.where((seen >> 4 == near[n] + z * NC) & parent, at - AT_PAR, 0)
        got = jnp.max(v, axis=2, keepdims=True)
        sent = jnp.where(at == n, got, sent)
    asks[PEERS:PEERS + NZ] = jnp.where(
        parent, ((x - (seen >> 9)) & 3) * 2 + ((core - (seen >> 4)) & 1), sent)
    to_smem = pltpu.make_async_copy(asks, idx_smem, local_sem)
    to_smem.start()
    to_smem.wait()

    def relay_copy(n, g):
        return pltpu.make_async_remote_copy(
            src_ref=relay_send.at[n, pl.ds(4 * g, 4)], dst_ref=up_recv.at[n, pl.ds(4 * g, 4)],
            send_sem=b_ss.at[B_UP], recv_sem=b_rs.at[B_UP],
            device_id={"brick": near[n] + z * NC}, device_id_type=MESH,
        )

    for g in range(NZ // 4):
        for j in range(4 * g, 4 * g + 4):
            if j:
                column_copy(j).wait_recv()
        for j in range(4 * g, 4 * g + 4):
            children = [column[j, b] for b in range(4)]
            up_recv[0, j] = choose(children, idx_smem[PEERS + j, 0, 0])
            for n in range(1, 8):
                relay_send[n, j] = choose(children, idx_smem[PEERS + j, 0, n])
        for n in range(1, 8):
            relay_copy(n, g).start()

    up_done = pltpu.make_async_remote_copy(
        src_ref=relay_send.at[pl.ds(1, 7)], dst_ref=up_recv.at[pl.ds(1, 7)],
        send_sem=b_ss.at[B_UP], recv_sem=b_rs.at[B_UP],
        device_id={"brick": near[1] + z * NC}, device_id_type=MESH,
    )
    up_done.wait_recv()
    row = lax.broadcasted_iota(jnp.int32, (256, 128), 0)
    lane = lax.broadcasted_iota(jnp.int32, (256, 128), 1)
    same = row % 16 == lane % 16
    wide = lax.broadcasted_iota(jnp.int32, (1, 128), 1) // 16

    def add_children(g, acc):
        codes = jnp.zeros((1, 128), jnp.int32)
        for i in range(8):
            codes = jnp.where(wide == i, idx_smem[8 * (g % 2 * 8 + i) + g // 2, 0, 4], codes)
        hot = jnp.where(same & (row // 16 == codes), 1.0, 0.0).astype(BF16)
        return acc + nn(hot, up_recv[g // 2, pl.ds(g % 2 * 8, 8)].reshape(128, 128))

    summed = lax.fori_loop(0, PEERS // 8, add_children, jnp.zeros((256, 128), F32))
    coarse_all[y] = summed.astype(BF16).reshape(2, 128, 128)

    def in_halves(ref, first, second):
        copies = []
        for phase, half in ((first, y // 3), (second, 1 - y // 3)):
            part = ref.at[y, :, pl.ds(pl.multiple_of(64 * half, 64), 64), :]
            copies.append(y_copies(phase, lambda p, part=part: part, part))
            y_start(copies[-1])
        y_arrived(copies[0])
        return copies

    gather = in_halves(coarse_all, Y_CG, Y_CG2)
    gather_weights((Y_UP, up_w, up_all), (Y_FW, fine_w, fine_w_all))

    def halo(bricks, whole, pieces, f_field, link_row, f_phase, r_phase, y_phase,
             f_send, r_send, f_recv, r_recv, halo_all, inner, outer, rows, halves, meanwhile):
        for b in range(bricks):
            source = jnp.concatenate(
                [whole[0, b, 0:64, :], whole[NY - 1, b, 64:128, :], whole[y, b]], axis=0)
            found = nn(pieces[...], source)
            faces[pl.ds(6 * b, 6)] = found[:96].astype(BF16).reshape(6, 16, 128)
            for r in range(20):
                rims[20 * b + r] = found[96 + 2 * r:98 + 2 * r].astype(BF16)

        def answer(j, back):
            for n in range(8):
                asker = 8 * back + (NX - n // 2) % NX * 2 + n % 2
                f_send[8 * j + n] = faces[within(idx_smem[asker, 0, f_field], 6 * bricks)]
                r_send[8 * j + n] = rims[within(idx_smem[asker, 0, f_field + 1], 20 * bricks)]

        exchange(((f_phase, lambda s: f_send.at[s], f_recv), (r_phase, lambda s: r_send.at[s], r_recv)),
                 answer)
        f_recv[0] = f_send[0]
        r_recv[0] = r_send[0]
        meanwhile()
        y_arrived(halves[1])
        for b in range(bricks):
            source = jnp.concatenate([whole[i, b] for i in range(NY)], axis=0)
            frame[b, 0:rows, :] = nn(inner[...], source)
        waits = [b_all(f_phase, f_send, f_recv), b_all(r_phase, r_send, r_recv)]
        for w in waits:
            w.wait_recv()
        for b in range(bricks):
            for k in range(6):
                halo_all[y, b, 16 * k:16 * k + 16, :] = f_recv[within(table[link_row, 0, 26 * b + k], PEERS + 1)]
            for r in range(20):
                rim_rows[b, 2 * r:2 * r + 2, :] = r_recv[within(table[link_row, 0, 26 * b + 6 + r], PEERS + 1)].astype(F32)
            halo_all[y, b, 96:144, :] = rim_rows[b].astype(BF16)
        around = y_copies(y_phase, lambda p: mine(halo_all), mine(halo_all))
        y_start(around)
        y_arrived(around)
        for b in range(bricks):
            source = jnp.concatenate([halo_all[i, b] for i in range(NY)], axis=0)
            frame[b, 0:rows, :] = frame[b, 0:rows, :] + nn(outer[...], source)
        return waits, around

    def conv(bricks, planes, starts, weights, bias_row):
        for tap in range(27):
            a, a2, a3 = tap // 9, (tap // 3) % 3, tap % 3
            for b in range(bricks):
                for n, start in enumerate(starts):
                    at = ((a3 * planes + start + a) * 10 + a2) * 8
                    columns[(2 * b + n) * 64:(2 * b + n + 1) * 64, tap * 128:tap * 128 + 128] = (
                        frame[b, at:at + 64, :].astype(BF16))
        whole = nt(columns[0:bricks * 128, :], weights[...])
        shift = bias_all[0] + bias_all[1] + bias_all[2] + bias_all[3]
        return jnp.maximum(whole + shift[bias_row:bias_row + 1, :], 0.0)

    def flatten_weights():
        for copies in later:
            y_arrived(copies)
        for tap in range(27):
            for i in range(NY):
                for src, dst in ((coarse_w_all, coarse_w_flat), (fine_w_all, fine_w_flat)):
                    dst[32 * i:32 * i + 32, tap * 128:tap * 128 + 128] = src[i, tap]
        pick(fine_pick, ROW_FP, 0, 256)
        pick(fine_inner, ROW_FF, 0, 512)
        pick(fine_outer, ROW_FF, 512, 4 * HALO)

    coarse_waits, coarse_around = halo(
        2, coarse_all, coarse_pick, 2, 1, B_CF, B_CR, Y_CH,
        cf_send, cr_send, cf_recv, cr_recv, coarse_halo, coarse_inner, coarse_outer, 1440,
        gather, flatten_weights)
    coarse_out = conv(2, 6, (0, 3), coarse_w_flat, 0).astype(BF16)
    for p in range(2):
        for n in range(2):
            at = (2 * p + n) * 64
            octants[pl.ds(8 * p + 4 * n, 4)] = (
                nn(octant[...], coarse_out[at:at + 64]).astype(BF16).reshape(4, 16, 128))

    def plane_copy(n, g):
        return pltpu.make_async_remote_copy(
            src_ref=down_send.at[n, pl.ds(4 * g, 4)], dst_ref=down_mid.at[n, pl.ds(4 * g, 4)],
            send_sem=d_ss.at[g], recv_sem=d_rs.at[g],
            device_id={"brick": near[n] + z * NC}, device_id_type=MESH,
        )

    def plane_all(g):
        return pltpu.make_async_remote_copy(
            src_ref=down_send.at[pl.ds(1, 7), pl.ds(4 * g, 4)],
            dst_ref=down_mid.at[pl.ds(1, 7), pl.ds(4 * g, 4)],
            send_sem=d_ss.at[g], recv_sem=d_rs.at[g],
            device_id={"brick": near[1] + z * NC}, device_id_type=MESH,
        )

    def back_of(j):
        return j if j in (0, NZ - 1) else j + 1 if j % 2 else j - 1

    for g in range(NZ // 4 - 1, -1, -1):
        for j in range(4 * g, 4 * g + 4):
            for n in range(8):
                asker = 8 * back_of(j) + (NX - n // 2) % NX * 2 + n % 2
                found = octants[within(idx_smem[asker, 0, 4], 16)]
                if n:
                    down_send[n, j] = found
                else:
                    down_mid[0, j] = found
        for n in range(1, 8):
            plane_copy(n, g).start()
    for g in range(NZ // 4 - 1, -1, -1):
        plane_all(g).wait_recv()
        for j in range(4 * g, 4 * g + 4):
            arrived = [down_mid[n, j] for n in range(8)]
            for b in range(4):
                down_out[j, b] = choose(arrived, idx_smem[PEERS + back_of(j), 0, AT_PAR + b])
        for j in range(4 * g + 3, 4 * g - 1, -1):
            if j:
                pltpu.make_async_remote_copy(
                    src_ref=down_out.at[j], dst_ref=down_recv.at[j], send_sem=b_ss.at[B_DOWN],
                    recv_sem=b_rs.at[B_DOWN], device_id={"brick": near[0] + z_base(j)},
                    device_id_type=MESH,
                ).start()
    down_recv[0] = down_out[0]
    down_done = pltpu.make_async_remote_copy(
        src_ref=down_out.at[pl.ds(1, NZ - 1)], dst_ref=down_recv.at[pl.ds(1, NZ - 1)],
        send_sem=b_ss.at[B_DOWN], recv_sem=b_rs.at[B_DOWN],
        device_id={"brick": near[0] + z_base(1)}, device_id_type=MESH,
    )
    down_done.wait_recv()
    coarse_rows = jnp.concatenate([down_recv[within(table[1, 0, AT_PAR + b], NZ), b] for b in range(4)], axis=0)
    for o in range(8):
        weight = jnp.concatenate([up_all[i, o] for i in range(NY)], axis=0)
        lifted = nt(coarse_rows, weight)
        for b in range(4):
            merged_all[y, b, 16 * o:16 * o + 16, :] = (
                own[b, 16 * o:16 * o + 16, :].astype(F32) + lifted[16 * b:16 * b + 16]).astype(BF16)
    merge = in_halves(merged_all, Y_MG, Y_MG2)

    fine_waits, fine_around = halo(
        4, merged_all, fine_pick, 0, 0, B_FF, B_FR, Y_FH,
        ff_send, fr_send, ff_recv, fr_recv, fine_halo, fine_inner, fine_outer, 960,
        merge, lambda: None)
    refined = conv(4, 4, (0, 1), fine_w_flat, 1)
    for b in range(4):
        out_send[b] = refined[128 * b:128 * b + 128].T.astype(BF16)
    back = y_copies(Y_OUT, lambda p: out_send.at[:, pl.ds(pl.multiple_of(p * 32, 32), 32), :],
                    mine(out_recv))
    y_start(back)
    out_recv[y] = out_send[:, pl.ds(pl.multiple_of(y * 32, 32), 32), :]
    y_arrived(back)
    for i in range(NY):
        out[:, :, 128 * i:128 * i + 128] = out_recv[i]

    for w in idx_waits + [up_done, down_done] + coarse_waits + fine_waits:
        w.wait_send()
    for j in range(1, NZ):
        column_copy(j).wait_send()
    for g in range(NZ // 4):
        plane_all(g).wait_send()
    for copies in [feat_copies, down_copies, coarse_around, fine_around, back] + gather + merge + later:
        for c in copies:
            c.wait_send()


def per_device(features, fine_links, coarse_links, parents, down_weight, coarse_weight, up_weight,
               fine_weight, coarse_bias, fine_bias):
    y = lax.axis_index("chan")
    blank = lambda n: jnp.full((n,), -1, jnp.int32)
    link_rows = jnp.concatenate([
        fine_links.reshape(-1), blank(24), coarse_links.reshape(-1), parents, blank(72)])
    link_rows = link_rows.reshape(2, 1, 128)
    rows = lax.dynamic_index_in_dim(jnp.asarray(row_tables()), y, 0, keepdims=False)
    bias = jnp.stack([coarse_bias, fine_bias])
    bias = lax.dynamic_update_slice(jnp.zeros((8, 128), F32), bias, (0, y * 32))
    args = (
        link_rows, features, link_rows,
        jnp.transpose(down_weight, (0, 2, 1)), up_weight, coarse_weight, fine_weight, bias,
        jnp.broadcast_to(rows[:, None], (ROWS, 128)),
    )
    v = pltpu.VMEM
    scratch = dict(
        notes=v((2, 1, 128), jnp.int32), table=pltpu.SMEM((2, 1, 128), jnp.int32), asks=v((144, 1, 128), jnp.int32),
        idx_smem=pltpu.SMEM((144, 1, 128), jnp.int32), unfold=v((128, 128), BF16),
        octant=v((64, 64), BF16), coarse_pick=v((HALO, 256), BF16), fine_pick=v((HALO, 256), BF16),
        coarse_inner=v((1440, 512), BF16), coarse_outer=v((1440, 4 * HALO), BF16),
        fine_inner=v((960, 512), BF16), fine_outer=v((960, 4 * HALO), BF16),
        coarse_w_flat=v((128, 3456), BF16), fine_w_flat=v((128, 3456), BF16),
        il_recv=v((128, 1, 128), jnp.int32), ir_recv=v((128, 1, 128), jnp.int32),
        feats=v((4, 128, 128), BF16), down_all=v((4, 8, 32, 128), BF16), bias_all=v((4, 8, 128), F32),
        up_all=v((4, 8, 32, 128), BF16), coarse_w_all=v((4, 27, 32, 128), BF16),
        fine_w_all=v((4, 27, 32, 128), BF16), own=v((4, 128, 128), BF16), child=v((4, 16, 128), BF16),
        column=v((16, 4, 16, 128), BF16), relay_send=v((8, 16, 16, 128), BF16),
        up_recv=v((8, 16, 16, 128), BF16),
        coarse_all=v((4, 2, 128, 128), BF16), faces=v((24, 16, 128), BF16), rims=v((80, 2, 128), BF16),
        cf_send=v((128, 16, 128), BF16), cr_send=v((128, 2, 128), BF16),
        cf_recv=v((129, 16, 128), BF16), cr_recv=v((129, 2, 128), BF16),
        coarse_halo=v((4, 2, HALO, 128), BF16), frame=v((4, 1440, 128), F32),
        columns=v((512, 3456), BF16), octants=v((16, 16, 128), BF16),
        down_send=v((8, 16, 16, 128), BF16), down_mid=v((8, 16, 16, 128), BF16),
        down_out=v((16, 4, 16, 128), BF16), down_recv=v((16, 4, 16, 128), BF16),
        merged_all=v((4, 4, 128, 128), BF16),
        ff_send=v((128, 16, 128), BF16), fr_send=v((128, 2, 128), BF16),
        ff_recv=v((129, 16, 128), BF16), fr_recv=v((129, 2, 128), BF16),
        fine_halo=v((4, 4, HALO, 128), BF16), rim_rows=v((4, 48, 128), F32),
        out_send=v((4, 128, 128), BF16), out_recv=v((4, 4, 32, 128), BF16),
        y_ss=pltpu.SemaphoreType.DMA((13, 3)), y_rs=pltpu.SemaphoreType.DMA((13, 3)),
        b_ss=pltpu.SemaphoreType.DMA((8,)), b_rs=pltpu.SemaphoreType.DMA((8,)),
        a_ss=pltpu.SemaphoreType.DMA((16,)), a_rs=pltpu.SemaphoreType.DMA((16,)),
        d_ss=pltpu.SemaphoreType.DMA((4,)), d_rs=pltpu.SemaphoreType.DMA((4,)),
        local_sem=pltpu.SemaphoreType.DMA,
    )
    return pl.pallas_call(
        kernel,
        out_shape=jax.ShapeDtypeStruct((4, 32, 512), BF16),
        in_specs=[pl.BlockSpec(memory_space=pltpu.SMEM)] + [pl.BlockSpec(memory_space=v)] * 8,
        out_specs=pl.BlockSpec(memory_space=v),
        scratch_shapes=list(scratch.values()),
        compiler_params=pltpu.CompilerParams(collective_id=0, has_side_effects=True),
    )(*args)


def solution(mesh):
    in_specs = (
        P("brick", "chan", None), P("brick", None), P("brick", None), P("brick"),
        P(None, None, "chan"), P(None, "chan", None), P(None, "chan", None), P(None, "chan", None),
        P("chan"), P("chan"),
    )
    return jax.shard_map(
        per_device, mesh=mesh, in_specs=in_specs, out_specs=P("brick", "chan", None), check_vma=False
    )
```

time: 218 us -> 170 us (0.78)
  Pallas kernels: 195 us -> 162 us
  other arithmetic: 14.8 us -> 0.68 us
    pallas_call x1, Pallas kernels: 195 us -> 162 us  [per_device(): pl.pallas_call(kernel, out_shape=jax.ShapeDtypeStruct((4, 32, 512), BF16)...]
    convert_element_type x8 -> x0, other arithmetic: 9.78 us -> none  [picks(): return (rows[..., None] == jnp.arange(width, dtype=jnp.int32)).astype(BF16)]
    add x6 -> x0, other arithmetic: 3.63 us -> none  [the longest x4 2.91 us: requests(): wanted = (links % per_owner * links.shape[1] + number).reshape(1, -1)]
where the time goes in v1:
time: 170 us
  Pallas kernels  162 us (95%)
  local copies, waits for them, and re-layouts  7.71 us (5%)
    pallas_call x1, Pallas kernels, per_device(): pl.pallas_call(kernel, out_shape=jax.ShapeDtypeStruct((4, 32, 512), BF16)...  162 us

profile of v1, /device:TPU:1, one launch (start us, length us, event | category | flops | bytes accessed | tf_op | source)
XLA Modules:
  0.0 170.1 jit_solution(4573950519725418550)
XLA Ops:
  0.0 0.8 reshape.11
  0.8 0.8 reshape.12
  1.5 1.3 concatenate.3
  2.8 0.7 pad_maximum_fusion
  3.5 0.3 dynamic_update_slice.3.bias
  3.8 0.0 copy-start
  3.8 0.8 dynamic-slice_reduce_fusion
  4.7 2.2 %broadcast_in_dim.17.row_of = s32[2880,128]{1,0:T(8,128)} broadcast(s32[2880]{0:T(1024)S(1)} %dynamic-slice_reduce_fusion), dimensions={0} | broadcast | bytes 1486080 | tf_op jit(solution)/shard_map/broadcast_in_dim | solution.py:586
  6.8 0.0 copy-done
  6.8 161.7 %shard_map.109 = bf16[4,32,512]{2,1,0:T(8,128)(2,1)} custom-call(s32[2,1,128]{2,1,0:T(1,128)} %bitcast.5, bf16[4,32,512]{2,1,0:T(8,128)(2,1)} %feat.1, s32[2,1,128]{2,1,0:T(1,128)} %bitcast.6, bf16[8,32,128]{2,1,0:T(8,128)(2,1)} %bitcast.4, bf16[8,32,128]{2,1,0:T(8,128)(2,1)} %up_w.1, bf16[27,32,128]{2,1,0:T(8,128)(2,1)} %coarse_w.1, ...), custom_call_target="tpu_custom_call" | custom-call | tf_op jit(solution)/shard_map/pallas_call | solution.py:620
  168.5 1.6 copy.14
  (3 shorter events, 0.0 us)
Async XLA Ops:
  3.8 3.0 %copy-start = (f32[8,128]{1,0:T(8,128)}, f32[8,128]{1,0:T(8,128)S(1)}, u32[]{:S(2)}) copy-start(f32[8,128]{1,0:T(8,128)S(1)} %dynamic_update_slice.3.bias) | copy-start | bytes 12292

commit v2 on v1

--- a/solution.py
+++ b/solution.py
@@ -133,7 +133,7 @@
 
 AT_PAR = 52
 
-Y_FEAT, Y_DOWN, Y_BIAS, Y_UP, Y_CW, Y_FW, Y_CG, Y_CG2, Y_CH, Y_MG, Y_MG2, Y_FH, Y_OUT = range(13)
+Y_FEAT, Y_DOWN, Y_BIAS, Y_UP, Y_CW, Y_FW, Y_CG, Y_CG2, Y_CH, Y_CR, Y_MG, Y_MG2, Y_FH, Y_FR, Y_OUT = range(15)
 B_IDX, B_IDR, B_UP, B_CF, B_CR, B_DOWN, B_FF, B_FR = range(8)
 
 
@@ -436,16 +436,23 @@
             source = jnp.concatenate([whole[i, b] for i in range(NY)], axis=0)
             frame[b, 0:rows, :] = nn(inner[...], source)
         waits = [b_all(f_phase, f_send, f_recv), b_all(r_phase, r_send, r_recv)]
-        for w in waits:
-            w.wait_recv()
+        face_part, rim_part = halo_all.at[y, :, 0:96, :], halo_all.at[y, :, 96:HALO, :]
+        waits[0].wait_recv()
         for b in range(bricks):
             for k in range(6):
-                halo_all[y, b, 16 * k:16 * k + 16, :] = f_recv[within(table[link_row, 0, 26 * b + k], PEERS + 1)]
+                slot = within(table[link_row, 0, 26 * b + k], PEERS + 1)
+                halo_all[y, b, 16 * k:16 * k + 16, :] = f_recv[slot]
+        around = y_copies(y_phase, lambda p: face_part, face_part)
+        y_start(around)
+        waits[1].wait_recv()
+        for b in range(bricks):
             for r in range(20):
-                rim_rows[b, 2 * r:2 * r + 2, :] = r_recv[within(table[link_row, 0, 26 * b + 6 + r], PEERS + 1)].astype(F32)
-            halo_all[y, b, 96:144, :] = rim_rows[b].astype(BF16)
-        around = y_copies(y_phase, lambda p: mine(halo_all), mine(halo_all))
-        y_start(around)
+                slot = within(table[link_row, 0, 26 * b + 6 + r], PEERS + 1)
+                rim_rows[b, 2 * r:2 * r + 2, :] = r_recv[slot].astype(F32)
+            halo_all[y, b, 96:HALO, :] = rim_rows[b].astype(BF16)
+        rims_around = y_copies(y_phase + 1, lambda p: rim_part, rim_part)
+        y_start(rims_around)
+        around = around + rims_around
         y_arrived(around)
         for b in range(bricks):
             source = jnp.concatenate([halo_all[i, b] for i in range(NY)], axis=0)
@@ -611,7 +618,7 @@
         ff_recv=v((129, 16, 128), BF16), fr_recv=v((129, 2, 128), BF16),
         fine_halo=v((4, 4, HALO, 128), BF16), rim_rows=v((4, 48, 128), F32),
         out_send=v((4, 128, 128), BF16), out_recv=v((4, 4, 32, 128), BF16),
-        y_ss=pltpu.SemaphoreType.DMA((13, 3)), y_rs=pltpu.SemaphoreType.DMA((13, 3)),
+        y_ss=pltpu.SemaphoreType.DMA((15, 3)), y_rs=pltpu.SemaphoreType.DMA((15, 3)),
         b_ss=pltpu.SemaphoreType.DMA((8,)), b_rs=pltpu.SemaphoreType.DMA((8,)),
         a_ss=pltpu.SemaphoreType.DMA((16,)), a_rs=pltpu.SemaphoreType.DMA((16,)),
         d_ss=pltpu.SemaphoreType.DMA((4,)), d_rs=pltpu.SemaphoreType.DMA((4,)),

time: 170 us -> 171 us (level)
  no operation moved by 1% of the time
where the time goes in v2:
time: 171 us; the launch traced here: 170 us
  Pallas kernels  162 us (95%)
  local copies, waits for them, and re-layouts  7.71 us (5%)
    pallas_call x1, Pallas kernels, per_device(): pl.pallas_call(kernel, out_shape=jax.ShapeDtypeStruct((4, 32, 512), BF16)...  162 us

profile of v2, /device:TPU:1, one launch (start us, length us, event | category | flops | bytes accessed | tf_op | source)
XLA Modules:
  0.0 170.4 jit_solution(12035330871222741748)
XLA Ops:
  0.0 0.8 reshape.11
  0.8 0.8 reshape.12
  1.5 1.3 concatenate.3
  2.8 0.7 pad_maximum_fusion
  3.5 0.3 dynamic_update_slice.3.bias
  3.8 0.0 copy-start
  3.8 0.8 dynamic-slice_reduce_fusion
  4.7 2.2 %broadcast_in_dim.17.row_of = s32[2880,128]{1,0:T(8,128)} broadcast(s32[2880]{0:T(1024)S(1)} %dynamic-slice_reduce_fusion), dimensions={0} | broadcast | bytes 1486080 | tf_op jit(solution)/shard_map/broadcast_in_dim | solution.py:593
  6.8 0.0 copy-done
  6.8 162.0 %shard_map.109 = bf16[4,32,512]{2,1,0:T(8,128)(2,1)} custom-call(s32[2,1,128]{2,1,0:T(1,128)} %bitcast.5, bf16[4,32,512]{2,1,0:T(8,128)(2,1)} %feat.1, s32[2,1,128]{2,1,0:T(1,128)} %bitcast.6, bf16[8,32,128]{2,1,0:T(8,128)(2,1)} %bitcast.4, bf16[8,32,128]{2,1,0:T(8,128)(2,1)} %up_w.1, bf16[27,32,128]{2,1,0:T(8,128)(2,1)} %coarse_w.1, ...), custom_call_target="tpu_custom_call" | custom-call | tf_op jit(solution)/shard_map/pallas_call | solution.py:627
  168.8 1.6 copy.14
  (3 shorter events, 0.0 us)
Async XLA Ops:
  3.8 3.0 %copy-start = (f32[8,128]{1,0:T(8,128)}, f32[8,128]{1,0:T(8,128)S(1)}, u32[]{:S(2)}) copy-start(f32[8,128]{1,0:T(8,128)S(1)} %dynamic_update_slice.3.bias) | copy-start | bytes 12292
